TPU v7x, 32 devices: a whole 2x2x4 slice. The times are simulated.
32 devices in a mesh: expert: 2 (over x), dp: 16 (over z, y, core).
Axes of the slice: x: 2, y: 2, z: 4, core: 2. Of those that a mesh axis runs over, the one named last changes fastest.
Arguments:
- tokens: bfloat16 [256, 4096], P(('expert', 'dp')), may hold values from -6 to 6
- expert_ids: int32 [256, 2], P(('expert', 'dp')), may hold values from 0 to 1, as said below
- slots: int32 [256, 2], P(('expert', 'dp')), may hold values from -1 to 1, as said below
- mix_weights: float32 [256, 2], P(('expert', 'dp')), may hold values from 0.1 to 1
- w_gate: bfloat16 [2, 4096, 8192], P('expert', None, 'dp'), may hold values from -0.09375 to 0.09375
- w_up: bfloat16 [2, 4096, 8192], P('expert', None, 'dp'), may hold values from -0.09375 to 0.09375
- w_down: bfloat16 [2, 8192, 4096], P('expert', None, 'dp'), may hold values from -0.0625 to 0.0625
Outputs:
- mixed: bfloat16 [256, 4096], P(('expert', 'dp'))
Inputs may be any that keep to these rules, and one draw needn't show every extreme that they name: `expert_ids`: each token names 2 different experts. Within each aligned block of 8 tokens (the tokens of one device), the assignments to one expert get distinct slots among 0 to 1 in some order, at most 2 of them are kept and the others get -1; an expert with 2 or more assignments in the block has all 2 slots used. No two assignments of one block share an expert and a slot. In every block some expert has all 2 slots used.
All inputs are finite; a program needn't handle non-finite values.
Results may differ from a plain program's by a relative error of at most 0.0085.
Values may be sent and summed in bfloat16 or wider, within the bound.
A program may use at most 128 MiB of HBM per device.

v0:
```python
import jax
import jax.numpy as jnp
from jax import lax
from jax.sharding import PartitionSpec as P

CAP = 2


def shards(tokens, expert_ids, slots, mix_weights, w_gate, w_up, w_down):
    tok_rows, model_width = tokens.shape
    experts = lax.axis_size("expert")
    capacity = CAP
    slot_count = experts * capacity
    slot_ids = jnp.arange(slot_count, dtype=jnp.int32)
    slot_expert = slot_ids // capacity
    slot_index = slot_ids % capacity
    matches = (expert_ids[None, :, :] == slot_expert[:, None, None]) & (
        slots[None, :, :] == slot_index[:, None, None]
    )
    occupied = jnp.any(matches, axis=2)
    dispatch_table = occupied.astype(jnp.bfloat16)
    outgoing = jnp.dot(dispatch_table, tokens, preferred_element_type=jnp.float32).astype(
        jnp.bfloat16
    )
    arrived = lax.all_to_all(outgoing, "expert", split_axis=0, concat_axis=0, tiled=True)
    gate_w = w_gate[0]
    up_w = w_up[0]
    down_w = w_down[0]
    portion = lax.all_gather(arrived, "dp", axis=0, tiled=True)
    gate_part = jnp.dot(portion, gate_w, preferred_element_type=jnp.float32)
    up_part = jnp.dot(portion, up_w, preferred_element_type=jnp.float32)
    hidden = (jax.nn.silu(gate_part) * up_part).astype(jnp.bfloat16)
    summed = jnp.dot(
        lax.all_gather(hidden, "dp", axis=1, tiled=True), down_w, preferred_element_type=jnp.float32
    )
    result = summed.astype(jnp.bfloat16)
    groups = lax.axis_size("dp")
    blocks = result.reshape(groups, experts, capacity, result.shape[1])
    blocks = lax.all_to_all(blocks, "expert", split_axis=1, concat_axis=1, tiled=True)
    blocks = lax.all_to_all(blocks, "dp", split_axis=0, concat_axis=3, tiled=True)
    returned = blocks.reshape(slot_count, model_width)
    weight_table = jnp.sum(jnp.where(matches, mix_weights[None, :, :], 0.0), axis=2)
    mixed = jnp.dot(
        weight_table.T,
        returned.astype(jnp.float32),
        precision=lax.Precision.HIGHEST,
        preferred_element_type=jnp.float32,
    )
    return mixed.astype(jnp.bfloat16)


def solution(mesh):
    placed = (
        P(("expert", "dp"), None),
        P(("expert", "dp"), None),
        P(("expert", "dp"), None),
        P(("expert", "dp"), None),
        P("expert", None, "dp"),
        P("expert", None, "dp"),
        P("expert", None, "dp"),
    )
    return jax.shard_map(
        shards, mesh=mesh, in_specs=placed, out_specs=P(("expert", "dp"), None), check_vma=False
    )
```

profile of v0, /device:TPU:0, one launch (start us, length us, event | category | flops | bytes accessed | tf_op | source)
XLA Modules:
  0.0 106.0 jit_solution(6045944678401223639)
XLA Ops:
  6.5 0.0 copy-start
  6.5 0.0 all-gather.3.cloned.1.call-start
  6.5 0.8 fusion.15
  7.4 0.0 copy-done
  7.4 0.1 convolution_convert_fusion.1
  7.6 8.0 %all_to_all.32 = bf16[2,2,4096]{2,1,0:T(2,128)(2,1)S(1)} all-to-all(bf16[2,2,4096]{2,1,0:T(2,128)(2,1)S(1)} %all_to_all.22), channel_id=1, replica_groups=mesh['expert'=2,'dp'=16] {'expert'}, dimensions={0} | all-to-all | bytes 65536 | tf_op jit(solution)/shard_map/all_to_all | solution.py:25
  15.6 23.2 %all-gather = bf16[16,4,4096]{2,1,0:T(4,128)(2,1)S(1)} all-gather(bf16[1,4,4096]{2,1,0:T(4,128)(2,1)S(1)} %reshape.36), channel_id=1, replica_groups=mesh['expert'=2,'dp'=16] {'dp'}, dimensions={0}, use_global_device_ids=true | all-gather | bytes 557056 | tf_op jit(solution)/shard_map/all_gather | solution.py:29
  38.8 0.1 reshape.37
  38.9 0.0 copy-start.1
  38.9 3.2 %fusion.4 = f32[64,512]{1,0:T(8,128)S(1)} fusion(bf16[64,4096]{1,0:T(8,128)(2,1)S(1)} %reshape.37, bf16[1,4096,512]{2,1,0:T(8,128)(2,1)} %param.11), kind=kOutput, calls=%fused_computation.6 | convolution fusion | flops 268435456 | bytes 4849664 | tf_op jit(solution)/shard_map/dot_general | solution.py:30
  42.1 0.3 copy-done.1
  42.3 0.0 copy-start.2
  42.3 1.5 %fusion.9 = bf16[64,512]{1,0:T(8,128)(2,1)} fusion(bf16[64,4096]{1,0:T(8,128)(2,1)S(1)} %reshape.37, bf16[1,4096,512]{2,1,0:T(8,128)(2,1)S(1)} %copy-done.1, f32[64,512]{1,0:T(8,128)S(1)} %fusion.4), kind=kOutput, calls=%fused_computation.9 | convolution fusion | flops 268632064 | bytes 4915200 | tf_op jit(solution)/shard_map/dot_general | solution.py:31
  43.8 0.0 all-gather.3.cloned.1.call-update
  43.8 32.9 %all-gather.3.cloned.1.call-done = bf16[64,8192]{1,0:T(8,128)(2,1)} async-done(((bf16[64,512]{1,0:T(8,128)(2,1)}), bf16[64,8192]{1,0:T(8,128)(2,1)}) %all-gather.3.cloned.1.call-update) | async-done | bytes 1048592 | tf_op jit(solution)/shard_map/all_gather | solution.py:34
  76.8 3.3 %fusion.12 = bf16[64,256]{1,0:T(8,128)(2,1)S(1)} fusion(bf16[64,8192]{1,0:T(8,128)(2,1)} %all-gather.3.cloned.1.call-done, bf16[1,8192,256]{2,1,0:T(8,128)(2,1)} %param.13), kind=kOutput, calls=%fused_computation.10 | convolution fusion | flops 268451840 | bytes 5275648 | tf_op jit(solution)/shard_map/dot_general | solution.py:33
  80.1 6.5 %all_to_all.33 = bf16[16,2,2,256]{3,2,0,1:T(2,128)(2,1)S(1)} all-to-all(bf16[16,2,2,256]{3,2,0,1:T(2,128)(2,1)S(1)} %copy.25), channel_id=1, replica_groups=mesh['expert'=2,'dp'=16] {'expert'}, dimensions={1} | all-to-all | bytes 65536 | tf_op jit(solution)/shard_map/all_to_all | solution.py:39
  86.6 0.6 copy.26
  87.2 4.3 %all-to-all-start.2 = ((bf16[16,2,2,256]{3,2,1,0:T(2,128)(2,1)}), bf16[16,2,2,256]{3,2,1,0:T(2,128)(2,1)S(1)}, u32[]{:S(2)}, u32[]{:S(2)}) async-start(bf16[16,2,2,256]{3,2,1,0:T(2,128)(2,1)} %copy.26), calls=%async_computation.2 | async-start | bytes 65536 | tf_op jit(solution)/shard_map/all_to_all | solution.py:40
  91.6 0.0 copy-done.2
  91.6 6.6 %all-to-all-done.2 = bf16[16,2,2,256]{3,2,1,0:T(2,128)(2,1)S(1)} async-done(((bf16[16,2,2,256]{3,2,1,0:T(2,128)(2,1)}), bf16[16,2,2,256]{3,2,1,0:T(2,128)(2,1)S(1)}, u32[]{:S(2)}, u32[]{:S(2)}) %all-to-all-start.2) | async-done | bytes 32800 | tf_op jit(solution)/shard_map/all_to_all | solution.py:40
  98.2 0.9 convolution_convert_fusion
  (8 shorter events, 0.1 us)
Async XLA Ops:
  6.5 0.8 copy-start
  6.5 70.2 %all-gather.3.cloned.1.call-start = ((), (), s32[]{:S(2)}) async-start(), calls=%async_computation.3 | async-start | bytes 1114112 | tf_op jit(solution)/shard_map/all_gather | solution.py:34
  38.9 3.5 %copy-start.1 = (bf16[1,4096,512]{2,1,0:T(8,128)(2,1)S(1)}, bf16[1,4096,512]{2,1,0:T(8,128)(2,1)}, u32[]{:S(2)}) copy-start(bf16[1,4096,512]{2,1,0:T(8,128)(2,1)} %param.12) | copy-start | bytes 12582916
  42.3 49.2 %copy-start.2 = (f32[8,2]{0,1:T(2,128)S(1)}, f32[8,2]{0,1:T(2,128)}, u32[]{:S(2)}) copy-start(f32[8,2]{0,1:T(2,128)} %param.10) | copy-start | bytes 196
  87.2 11.0 %all-to-all-start.2 = ((bf16[16,2,2,256]{3,2,1,0:T(2,128)(2,1)}), bf16[16,2,2,256]{3,2,1,0:T(2,128)(2,1)S(1)}, u32[]{:S(2)}, u32[]{:S(2)}) async-start(bf16[16,2,2,256]{3,2,1,0:T(2,128)(2,1)} %copy.26), calls=%async_computation.2 | async-start | bytes 65536 | tf_op jit(solution)/shard_map/all_to_all | solution.py:40
Sparse Core Ops, SparseCore 0:
  44.0 32.7 all-gather.2
where the time goes:
time: 106 us
  waiting for transfers between devices  39.5 us (37%)
  blocking collectives  37.7 us (36%)
  between operations  13.5 us (13%)
  matrix products  8.99 us (8%)
  starting transfers between devices  4.33 us (4%)
  local copies, waits for them, and re-layouts  1.17 us (1%)
    all_gather x1, waiting for transfers between devices, shards(): lax.all_gather(hidden, 'dp', axis=1, tiled=True)  32.9 us
    all_gather x1, blocking collectives, shards(): portion = lax.all_gather(arrived, 'dp', axis=0, tiled=True)  23.2 us
    all_to_all x1, blocking collectives, shards(): lax.all_to_all(outgoing, 'expert', split_axis=0, concat_axis=0, tiled=True)  7.98 us
    all_to_all x1, waiting for transfers between devices, shards(): lax.all_to_all(blocks, 'dp', split_axis=0, concat_axis=3, tiled=True)  6.61 us
    all_to_all x1, blocking collectives, shards(): lax.all_to_all(blocks, 'expert', split_axis=1, concat_axis=1, tiled=True)  6.47 us
    all_to_all x1, starting transfers between devices, shards(): lax.all_to_all(blocks, 'dp', split_axis=0, concat_axis=3, tiled=True)  4.33 us
    dot_general x1, matrix products, shards(): jnp.dot(lax.all_gather(hidden, 'dp', axis=1, tiled=True), down_w, preferr...  3.31 us
    dot_general x1, matrix products, shards(): gate_part = jnp.dot(portion, gate_w, preferred_element_type=jnp.float32)  3.18 us
  transfers between devices with their start and end apart: 2, of which 2 were waited for; matrix products, arithmetic and copies ran while one was open for 0% of the time, Pallas kernels for 0%

commit v1 on v0

v1 whole, which is shorter than its diff:
```python
import functools

import jax
import jax.numpy as jnp
from jax import lax
from jax.experimental import pallas as pl
from jax.experimental.pallas import tpu as pltpu
from jax.sharding import PartitionSpec as P

CAP = 2
PLANE = 4
HALVES = 2
BF = jnp.bfloat16
F32 = jnp.float32


def collective_form(tokens, expert_ids, slots, mix_weights, w_gate, w_up, w_down):
    tok_rows, model_width = tokens.shape
    experts = lax.axis_size("expert")
    slot_count = experts * CAP
    slot_ids = jnp.arange(slot_count, dtype=jnp.int32)
    matches = (expert_ids[None, :, :] == (slot_ids // CAP)[:, None, None]) & (
        slots[None, :, :] == (slot_ids % CAP)[:, None, None]
    )
    table = jnp.any(matches, axis=2).astype(BF)
    outgoing = jnp.dot(table, tokens, preferred_element_type=F32).astype(BF)
    arrived = lax.all_to_all(outgoing, "expert", split_axis=0, concat_axis=0, tiled=True)
    portion = lax.all_gather(arrived, "dp", axis=0, tiled=True)
    gate_part = jnp.dot(portion, w_gate[0], preferred_element_type=F32)
    up_part = jnp.dot(portion, w_up[0], preferred_element_type=F32)
    hidden = (jax.nn.silu(gate_part) * up_part).astype(BF)
    summed = jnp.dot(
        lax.all_gather(hidden, "dp", axis=1, tiled=True), w_down[0], preferred_element_type=F32
    )
    result = summed.astype(BF)
    blocks = result.reshape(lax.axis_size("dp"), experts, CAP, result.shape[1])
    blocks = lax.all_to_all(blocks, "expert", split_axis=1, concat_axis=1, tiled=True)
    blocks = lax.all_to_all(blocks, "dp", split_axis=0, concat_axis=3, tiled=True)
    returned = blocks.reshape(slot_count, model_width)
    weight_table = jnp.sum(jnp.where(matches, mix_weights[None, :, :], 0.0), axis=2)
    mixed = jnp.dot(
        weight_table.T,
        returned.astype(F32),
        precision=lax.Precision.HIGHEST,
        preferred_element_type=F32,
    )
    return mixed.astype(BF)


def kernel(
    experts, groups,
    tok_ref, ids_ref, slot_ref, mix_ref, wg_hbm, wu_hbm, wd_hbm, out_ref,
    wg, wu, wd, obuf, ubuf, xbuf, hbuf, pbuf, rbuf,
    wsem, s1s, s1r, s2s, s2r, s3s, s3r, azs, azr, ays, ayr, acs, acr, rs, rr,
):
    planes = groups // PLANE
    units = experts * planes
    rows = units * CAP
    tok_rows, width = tok_ref.shape
    half = width // HALVES
    chunk_count = rows // CAP
    chunk = half // chunk_count
    cols = wd.shape[2]
    x = lax.axis_index("expert")
    d = lax.axis_index("dp")
    z, b = d // PLANE, d % PLANE
    y, c = b // 2, b % 2
    unit = x * planes + z
    y_block = (1 - y) * 2 + c
    c_block = y * 2 + 1 - c
    yc_block = (1 - y) * 2 + 1 - c

    def dev(xx, dd):
        return (xx, dd)

    def rdma(src, dst, ssem, rsem, device):
        return pltpu.make_async_remote_copy(
            src_ref=src, dst_ref=dst, send_sem=ssem, recv_sem=rsem,
            device_id=device, device_id_type=pl.DeviceIdType.MESH,
        )

    y_dev = dev(x, z * PLANE + y_block)
    c_dev = dev(x, z * PLANE + c_block)
    offsets = [(dx, dz) for dz in range(planes) for dx in range(experts) if dx or dz]

    def peer(dx, dz):
        return lax.rem(x + dx, experts), lax.rem(z + dz, planes)

    barrier = pltpu.get_barrier_semaphore()
    for dx, dz in offsets:
        px, pz = peer(dx, dz)
        pl.semaphore_signal(barrier, inc=1, device_id=dev(px, pz * PLANE + b),
                            device_id_type=pl.DeviceIdType.MESH)
    for other in (y_dev, c_dev):
        pl.semaphore_signal(barrier, inc=1, device_id=other,
                            device_id_type=pl.DeviceIdType.MESH)

    loads = []
    for h in range(HALVES):
        part = pl.ds(h * half, half)
        loads.append(pltpu.make_async_copy(wg_hbm.at[0, part], wg.at[part], wsem.at[2 * h]))
        loads.append(pltpu.make_async_copy(wu_hbm.at[0, part], wu.at[part], wsem.at[2 * h + 1]))
    depth = wd.shape[1]
    for g in range(groups):
        loads.append(pltpu.make_async_copy(
            wd_hbm.at[0, pl.ds(g * depth, depth)], wd.at[g], wsem.at[2 * HALVES + g]))
    for load in loads:
        load.start()

    ids = ids_ref[...]
    places = slot_ref[...]
    lanes = experts * chunk_count * CAP
    lane = lax.broadcasted_iota(jnp.int32, (tok_rows, 128), 1)
    lane_e, lane_r = lane // (chunk_count * CAP), lane % CAP
    hit = jnp.zeros((tok_rows, 128), F32)
    for k in range(ids.shape[1]):
        same = (ids[:, k:k + 1] == lane_e) & (places[:, k:k + 1] == lane_r)
        hit = jnp.where(same, 1.0, hit)
    tall = jnp.concatenate([hit] * chunk_count, axis=0)
    tall_row = lax.broadcasted_iota(jnp.int32, tall.shape, 0) // tok_rows
    tall_lane = (lax.broadcasted_iota(jnp.int32, tall.shape, 1) // CAP) % chunk_count
    pick = jnp.where(tall_row == tall_lane, tall, 0.0).T[:lanes].astype(BF)
    for h in range(HALVES):
        stack = jnp.concatenate(
            [tok_ref[:, h * half + j * chunk: h * half + (j + 1) * chunk].astype(F32)
             for j in range(chunk_count)], axis=0).astype(BF)
        sent = jnp.dot(pick, stack, preferred_element_type=F32).astype(BF)
        for e in range(experts):
            obuf[h, e] = sent[e * rows:(e + 1) * rows]
    weight_cols = {}
    mix = mix_ref[...]
    for e in range(experts):
        for r in range(CAP):
            total = jnp.zeros((tok_rows, 1), F32)
            for k in range(ids.shape[1]):
                total += jnp.where((ids[:, k:k + 1] == e) & (places[:, k:k + 1] == r),
                                   mix[:, k:k + 1], 0.0)
            weight_cols[e, r] = total

    pl.semaphore_wait(barrier, len(offsets) + 2)

    waits = []
    for h in range(HALVES):
        for n, (dx, dz) in reversed(list(enumerate(offsets))):
            px, pz = peer(dx, dz)
            copy = rdma(obuf.at[h, px], ubuf.at[h, unit], s1s.at[h, n], s1r.at[h, unit],
                        dev(px, pz * PLANE + b))
            copy.start()
            waits.append(copy)
    for h in range(HALVES):
        ubuf[h, unit] = obuf[h, x]

    count = units * chunk_count * CAP
    pr = lax.broadcasted_iota(jnp.int32, (count, count), 0)
    pc = lax.broadcasted_iota(jnp.int32, (count, count), 1)
    source = ((pr // CAP) % units) * (chunk_count * CAP) + (pr // rows) * CAP + pr % CAP
    order = jnp.where(pc == source, 1.0, 0.0).astype(BF)

    def arrival(buf, h, slot, rsem):
        return rdma(buf, buf, s2s.at[0], rsem, y_dev)

    gate = up = None
    for h in range(HALVES):
        for dx, dz in offsets:
            px, pz = peer(dx, dz)
            pu = px * planes + pz
            rdma(ubuf.at[h, pu], ubuf.at[h, pu], s1s.at[0, 0], s1r.at[h, pu], y_dev).wait_recv()
        arrived = ubuf[h].reshape(count, chunk)
        block = jnp.dot(order, arrived, preferred_element_type=F32).astype(BF)
        for j in range(chunk_count):
            xbuf[h, b, :, j * chunk:(j + 1) * chunk] = block[j * rows:(j + 1) * rows]
        mine = xbuf.at[h, b]
        to_y = rdma(mine, mine, s2s.at[h], s2r.at[h], y_dev)
        to_y.start()
        to_c = rdma(mine, mine, s3s.at[h, 0], s3r.at[h, 0], c_dev)
        to_c.start()
        waits += [to_y, to_c]
    for h in range(HALVES):
        theirs = xbuf.at[h, y_block]
        rdma(theirs, theirs, s2s.at[h], s2r.at[h], y_dev).wait_recv()
        forward = rdma(theirs, theirs, s3s.at[h, 1], s3r.at[h, 1], c_dev)
        forward.start()
        waits.append(forward)
        for n, blk in enumerate((c_block, yc_block)):
            got = xbuf.at[h, blk]
            rdma(got, got, s3s.at[h, n], s3r.at[h, n], c_dev).wait_recv()
        loads[2 * h].wait()
        loads[2 * h + 1].wait()
        part = pl.ds(h * half, half)
        slab = xbuf[h].reshape(PLANE * rows, half)
        g_part = jnp.dot(slab, wg[part], preferred_element_type=F32)
        u_part = jnp.dot(slab, wu[part], preferred_element_type=F32)
        gate = g_part if gate is None else gate + g_part
        up = u_part if up is None else up + u_part
    hidden = (gate / (1.0 + jnp.exp(-gate)) * up).astype(BF)
    hbuf[d] = hidden

    def dp_of(zz, blk):
        return zz * PLANE + blk

    shard = hbuf.at[d]
    for dz in range(planes - 1, 0, -1):
        pz = lax.rem(z + dz, planes)
        copy = rdma(shard, shard, azs.at[dz], azr.at[z], dev(x, dp_of(pz, b)))
        copy.start()
        waits.append(copy)
    copy = rdma(shard, shard, ays.at[0], ayr.at[z], y_dev)
    copy.start()
    waits.append(copy)
    copy = rdma(shard, shard, acs.at[0], acr.at[z, 0], c_dev)
    copy.start()
    waits.append(copy)
    for load in loads[2 * HALVES:]:
        load.wait()

    def product(g):
        return jnp.dot(hbuf[g], wd[g], preferred_element_type=F32)

    acc = product(d)
    for dz in range(planes):
        pz = lax.rem(z + dz, planes)
        if dz:
            g = dp_of(pz, b)
            got = hbuf.at[g]
            rdma(got, got, azs.at[dz], azr.at[pz], y_dev).wait_recv()
            on_y = rdma(got, got, ays.at[dz], ayr.at[pz], y_dev)
            on_y.start()
            on_c = rdma(got, got, acs.at[dz], acr.at[pz, 0], c_dev)
            on_c.start()
            waits += [on_y, on_c]
            acc += product(g)
        g = dp_of(pz, c_block)
        got = hbuf.at[g]
        rdma(got, got, acs.at[0], acr.at[pz, 0], c_dev).wait_recv()
        acc += product(g)
    for dz in range(planes):
        pz = lax.rem(z + dz, planes)
        g = dp_of(pz, y_block)
        got = hbuf.at[g]
        rdma(got, got, ays.at[0], ayr.at[pz], y_dev).wait_recv()
        on_c = rdma(got, got, acs.at[planes + dz], acr.at[pz, 1], c_dev)
        on_c.start()
        waits.append(on_c)
        acc += product(g)
    for dz in range(planes):
        pz = lax.rem(z + dz, planes)
        g = dp_of(pz, yc_block)
        got = hbuf.at[g]
        rdma(got, got, acs.at[0], acr.at[pz, 1], c_dev).wait_recv()
        acc += product(g)

    wide = cols // 128
    piece_rows = wide * CAP
    everyone = experts * groups
    result = acc.astype(BF)
    for w in range(wide):
        for p in range(everyone):
            pbuf[p, w * CAP:(w + 1) * CAP, :] = result[p * CAP:(p + 1) * CAP,
                                                       w * 128:(w + 1) * 128]
    me = x * groups + d

    def piece_of(device):
        dx, dd = device // groups, device % groups
        return (dd % PLANE) * units + dx * planes + dd // PLANE

    rbuf[me] = pbuf[piece_of(me)]
    for k in range(1, everyone):
        other = lax.rem(me + k, everyone)
        copy = rdma(pbuf.at[piece_of(other)], rbuf.at[me], rs.at[k], rr.at[me],
                    dev(other // groups, other % groups))
        copy.start()
        waits.append(copy)
    for k in range(1, everyone):
        other = lax.rem(me + k, everyone)
        rdma(rbuf.at[other], rbuf.at[other], rs.at[k], rr.at[other], y_dev).wait_recv()
    for g in range(groups):
        pieces = [rbuf[e * groups + g].astype(F32) for e in range(experts)]
        for w in range(wide):
            total = None
            for e in range(experts):
                for r in range(CAP):
                    term = weight_cols[e, r] * pieces[e][w * CAP + r:w * CAP + r + 1]
                    total = term if total is None else total + term
            out_ref[:, g * cols + w * 128:g * cols + (w + 1) * 128] = total.astype(BF)
    for copy in waits:
        copy.wait_send()


def kernel_form(tokens, expert_ids, slots, mix_weights, w_gate, w_up, w_down):
    experts, groups = lax.axis_size("expert"), lax.axis_size("dp")
    planes = groups // PLANE
    units = experts * planes
    rows = units * CAP
    tok_rows, width = tokens.shape
    hid = w_gate.shape[2]
    cols = w_down.shape[2]
    half = width // HALVES
    chunk_count = rows // CAP
    chunk = half // chunk_count
    everyone = experts * groups
    dma = pltpu.SemaphoreType.DMA
    return pl.pallas_call(
        functools.partial(kernel, experts, groups),
        out_shape=jax.ShapeDtypeStruct((tok_rows, width), BF),
        in_specs=[pl.BlockSpec(memory_space=pltpu.VMEM)] * 4
        + [pl.BlockSpec(memory_space=pl.ANY)] * 3,
        out_specs=pl.BlockSpec(memory_space=pltpu.VMEM),
        scratch_shapes=[
            pltpu.VMEM((width, hid), BF),
            pltpu.VMEM((width, hid), BF),
            pltpu.VMEM((groups, hid, cols), BF),
            pltpu.VMEM((HALVES, experts, rows, chunk), BF),
            pltpu.VMEM((HALVES, units, rows, chunk), BF),
            pltpu.VMEM((HALVES, PLANE, rows, half), BF),
            pltpu.VMEM((groups, PLANE * rows, hid), BF),
            pltpu.VMEM((everyone, cols // 128 * CAP, 128), BF),
            pltpu.VMEM((everyone, cols // 128 * CAP, 128), BF),
            dma((2 * HALVES + groups,)),
            dma((HALVES, units)), dma((HALVES, units)),
            dma((HALVES,)), dma((HALVES,)),
            dma((HALVES, 2)), dma((HALVES, 2)),
            dma((planes,)), dma((planes,)),
            dma((planes,)), dma((planes,)),
            dma((2 * planes,)), dma((planes, 2)),
            dma((everyone,)), dma((everyone,)),
        ],
        compiler_params=pltpu.CompilerParams(
            collective_id=0, has_side_effects=True, vmem_limit_bytes=56 * 2 ** 20
        ),
    )(tokens, expert_ids, slots, mix_weights, w_gate, w_up, w_down)


def solution(mesh):
    experts, groups = mesh.shape["expert"], mesh.shape["dp"]

    def shards(tokens, expert_ids, slots, mix_weights, w_gate, w_up, w_down):
        rows = experts * (groups // PLANE) * CAP
        fits = (
            groups % PLANE == 0
            and rows == 16
            and tokens.shape[0] % 8 == 0
            and tokens.shape[1] % (HALVES * (rows // CAP) * 128) == 0
            and w_gate.shape[2] % 128 == 0
            and w_down.shape[2] % 128 == 0
        )
        form = kernel_form if fits else collective_form
        return form(tokens, expert_ids, slots, mix_weights, w_gate, w_up, w_down)

    placed = (
        P(("expert", "dp"), None),
        P(("expert", "dp"), None),
        P(("expert", "dp"), None),
        P(("expert", "dp"), None),
        P("expert", None, "dp"),
        P("expert", None, "dp"),
        P("expert", None, "dp"),
    )
    return jax.shard_map(
        shards, mesh=mesh, in_specs=placed, out_specs=P(("expert", "dp"), None), check_vma=False
    )
```

time: 106 us -> 43.5 us (0.41)
  waiting for transfers between devices: 39.5 us -> 0 us
  Pallas kernels: 0 us -> 37.8 us
  blocking collectives: 37.7 us -> 0 us
  between operations: 13.5 us -> 0.01 us
  matrix products: 8.99 us -> 0 us
  local copies, waits for them, and re-layouts: 1.17 us -> 5.5 us
  starting transfers between devices: 4.33 us -> 0 us
    pallas_call x0 -> x1, Pallas kernels: none -> 37.8 us  [kernel_form(): pl.pallas_call(functools.partial(kernel, experts, groups), out_shape=jax....]
    all_gather x1 -> x0, waiting for transfers between devices: 32.9 us -> none  [shards(): lax.all_gather(hidden, 'dp', axis=1, tiled=True)]
    all_gather x1 -> x0, blocking collectives: 23.2 us -> none  [shards(): portion = lax.all_gather(arrived, 'dp', axis=0, tiled=True)]
    all_to_all x2 -> x0, blocking collectives: 14.4 us -> none  [the longest x1 7.98 us: shards(): lax.all_to_all(outgoing, 'expert', split_axis=0, concat_axis=0, tiled=True)]
    dot_general x5 -> x0, matrix products: 8.99 us -> none  [the longest x1 3.31 us: shards(): jnp.dot(lax.all_gather(hidden, 'dp', axis=1, tiled=True), down_w, preferr...]
    all_to_all x1 -> x0, waiting for transfers between devices: 6.61 us -> none  [shards(): lax.all_to_all(blocks, 'dp', split_axis=0, concat_axis=3, tiled=True)]
    unnamed x9 -> x4, local copies, waits for them, and re-layouts: 0.45 us -> 5.5 us
    all_to_all x1 -> x0, starting transfers between devices: 4.33 us -> none  [shards(): lax.all_to_all(blocks, 'dp', split_axis=0, concat_axis=3, tiled=True)]
  transfers between devices with their start and end apart: 2 -> 0, of which waited for: 2 -> 0; matrix products, arithmetic and copies ran while one was open for 0% -> 0% of each run, Pallas kernels for 0% -> 0%
where the time goes in v1:
time: 43.5 us; the launch traced here: 43.3 us
  Pallas kernels  37.8 us (87%)
  local copies, waits for them, and re-layouts  5.5 us (13%)
    pallas_call x1, Pallas kernels, kernel_form(): pl.pallas_call(functools.partial(kernel, experts, groups), out_shape=jax....  37.8 us
    unnamed x4, local copies, waits for them, and re-layouts  5.5 us

profile of v1, /device:TPU:0, one launch (start us, length us, event | category | flops | bytes accessed | tf_op | source)
XLA Modules:
  0.0 43.3 jit_solution(7748848158133714408)
XLA Ops:
  0.0 1.3 %copy.8.ids_ref = s32[8,2]{1,0:T(8,128)} copy(s32[8,2]{0,1:T(2,128)} %param.8) | data formatting | bytes 128 | tf_op args[1]
  1.3 1.3 %copy.9.slot_ref = s32[8,2]{1,0:T(8,128)} copy(s32[8,2]{0,1:T(2,128)} %param.9) | data formatting | bytes 128 | tf_op args[2]
  2.7 1.3 %copy.10.mix_ref = f32[8,2]{1,0:T(8,128)} copy(f32[8,2]{0,1:T(2,128)} %param.10) | data formatting | bytes 128 | tf_op args[3]
  4.0 37.8 %shard_map.73 = bf16[8,4096]{1,0:T(8,128)(2,1)} custom-call(bf16[8,4096]{1,0:T(8,128)(2,1)} %tok_ref.1, s32[8,2]{1,0:T(8,128)} %copy.8.ids_ref, s32[8,2]{1,0:T(8,128)} %copy.9.slot_ref, f32[8,2]{1,0:T(8,128)} %copy.10.mix_ref, bf16[1,4096,512]{2,1,0:T(8,128)(2,1)} %wg_hbm.1, bf16[1,4096,512]{2,1,0:T(8,128)(2,1)} %wu_hbm.1, bf16[1,8192,256]{2,1,0:T(8,128)(2,1)} %wd_hbm.1), custom_call_target="tpu_custom_call" | custom-call | tf_op jit(solution)/shard_map/pallas_call | solution.py:302
  41.8 1.5 %copy.12 = bf16[8,4096]{1,0:T(8,128)(2,1)} copy(bf16[8,4096]{1,0:T(8,128)(2,1)} %shard_map.73) | data formatting | bytes 131072

commit v2 on v1

--- a/solution.py
+++ b/solution.py
@@ -107,19 +107,22 @@
     for load in loads:
         load.start()
 
-    ids = ids_ref[...]
-    places = slot_ref[...]
     lanes = experts * chunk_count * CAP
-    lane = lax.broadcasted_iota(jnp.int32, (tok_rows, 128), 1)
-    lane_e, lane_r = lane // (chunk_count * CAP), lane % CAP
-    hit = jnp.zeros((tok_rows, 128), F32)
-    for k in range(ids.shape[1]):
-        same = (ids[:, k:k + 1] == lane_e) & (places[:, k:k + 1] == lane_r)
-        hit = jnp.where(same, 1.0, hit)
-    tall = jnp.concatenate([hit] * chunk_count, axis=0)
-    tall_row = lax.broadcasted_iota(jnp.int32, tall.shape, 0) // tok_rows
-    tall_lane = (lax.broadcasted_iota(jnp.int32, tall.shape, 1) // CAP) % chunk_count
-    pick = jnp.where(tall_row == tall_lane, tall, 0.0).T[:lanes].astype(BF)
+    ids = jnp.concatenate([ids_ref[...]] * (128 // tok_rows), axis=1)
+    places = jnp.concatenate([slot_ref[...]] * (128 // tok_rows), axis=1)
+    mix = jnp.concatenate([mix_ref[...]] * (128 // tok_rows), axis=1)
+    row = lax.broadcasted_iota(jnp.int32, (lanes, 128), 0)
+    row_e, row_j, row_r = row // rows, (row // CAP) % chunk_count, row % CAP
+    column_j = lax.broadcasted_iota(jnp.int32, (lanes, 128), 1) // tok_rows
+    pick = jnp.zeros((lanes, 128), F32)
+    table = jnp.zeros((8, 128), F32)
+    wide_row = lax.broadcasted_iota(jnp.int32, (8, 128), 0)
+    for k in range(ids_ref.shape[0]):
+        ids_k, places_k, mix_k = ids[k:k + 1], places[k:k + 1], mix[k:k + 1]
+        pick = jnp.where((ids_k == row_e) & (places_k == row_r) & (column_j == row_j), 1.0, pick)
+        table += jnp.where((ids_k == wide_row // CAP) & (places_k == wide_row % CAP), mix_k, 0.0)
+    pick = pick[:, :chunk_count * tok_rows].astype(BF)
+    table = table.T
     for h in range(HALVES):
         stack = jnp.concatenate(
             [tok_ref[:, h * half + j * chunk: h * half + (j + 1) * chunk].astype(F32)
@@ -127,15 +130,8 @@
         sent = jnp.dot(pick, stack, preferred_element_type=F32).astype(BF)
         for e in range(experts):
             obuf[h, e] = sent[e * rows:(e + 1) * rows]
-    weight_cols = {}
-    mix = mix_ref[...]
-    for e in range(experts):
-        for r in range(CAP):
-            total = jnp.zeros((tok_rows, 1), F32)
-            for k in range(ids.shape[1]):
-                total += jnp.where((ids[:, k:k + 1] == e) & (places[:, k:k + 1] == r),
-                                   mix[:, k:k + 1], 0.0)
-            weight_cols[e, r] = total
+    weight_cols = {(e, r): table[:tok_rows, e * CAP + r:e * CAP + r + 1]
+                   for e in range(experts) for r in range(CAP)}
 
     pl.semaphore_wait(barrier, len(offsets) + 2)
 
@@ -327,7 +323,7 @@
         compiler_params=pltpu.CompilerParams(
             collective_id=0, has_side_effects=True, vmem_limit_bytes=56 * 2 ** 20
         ),
-    )(tokens, expert_ids, slots, mix_weights, w_gate, w_up, w_down)
+    )(tokens, expert_ids.T, slots.T, mix_weights.T, w_gate, w_up, w_down)
 
 
 def solution(mesh):
@@ -338,7 +334,8 @@
         fits = (
             groups % PLANE == 0
             and rows == 16
-            and tokens.shape[0] % 8 == 0
+            and tokens.shape[0] == 8
+            and experts * CAP <= 8
             and tokens.shape[1] % (HALVES * (rows // CAP) * 128) == 0
             and w_gate.shape[2] % 128 == 0
             and w_down.shape[2] % 128 == 0

time: 43.5 us -> 39.5 us (0.908)
  local copies, waits for them, and re-layouts: 5.5 us -> 1.47 us
    unnamed x4 -> x1, local copies, waits for them, and re-layouts: 5.5 us -> 1.47 us
where the time goes in v2:
time: 39.5 us; the launch traced here: 39.3 us
  Pallas kernels  37.8 us (96%)
  local copies, waits for them, and re-layouts  1.47 us (4%)
    pallas_call x1, Pallas kernels, kernel_form(): pl.pallas_call(functools.partial(kernel, experts, groups), out_shape=jax....  37.8 us
    unnamed x1, local copies, waits for them, and re-layouts  1.47 us

profile of v2, /device:TPU:0, one launch (start us, length us, event | category | flops | bytes accessed | tf_op | source)
XLA Modules:
  0.0 39.3 jit_solution(185468160997343950)
XLA Ops:
  0.0 37.8 %shard_map.73 = bf16[8,4096]{1,0:T(8,128)(2,1)} custom-call(bf16[8,4096]{1,0:T(8,128)(2,1)} %tok_ref.1, s32[2,8]{1,0:T(2,128)} %bitcast.3, s32[2,8]{1,0:T(2,128)} %bitcast.4, f32[2,8]{1,0:T(2,128)} %bitcast.5, bf16[1,4096,512]{2,1,0:T(8,128)(2,1)} %wg_hbm.1, bf16[1,4096,512]{2,1,0:T(8,128)(2,1)} %wu_hbm.1, bf16[1,8192,256]{2,1,0:T(8,128)(2,1)} %wd_hbm.1), custom_call_target="tpu_custom_call" | custom-call | tf_op jit(solution)/shard_map/pallas_call | solution.py:298
  37.8 1.5 %copy.9 = bf16[8,4096]{1,0:T(8,128)(2,1)} copy(bf16[8,4096]{1,0:T(8,128)(2,1)} %shard_map.73) | data formatting | bytes 131072

commit v3 on v2

--- a/solution.py
+++ b/solution.py
@@ -9,6 +9,7 @@
 
 CAP = 2
 PLANE = 4
+PARTS = 1
 HALVES = 2
 BF = jnp.bfloat16
 F32 = jnp.float32
@@ -49,8 +50,8 @@
 
 def kernel(
     experts, groups,
-    tok_ref, ids_ref, slot_ref, mix_ref, wg_hbm, wu_hbm, wd_hbm, out_ref,
-    wg, wu, wd, obuf, ubuf, xbuf, hbuf, pbuf, rbuf,
+    tok_hbm, ids_hbm, slot_hbm, mix_hbm, wg_hbm, wu_hbm, wd_hbm, out_ref,
+    tok_ref, ids_ref, slot_ref, mix_ref, tsem, wg, wu, wd, obuf, ubuf, xbuf, hbuf, pbuf, rbuf,
     wsem, s1s, s1r, s2s, s2r, s3s, s3r, azs, azr, ays, ayr, acs, acr, rs, rr,
 ):
     planes = groups // PLANE
@@ -82,6 +83,10 @@
     y_dev = dev(x, z * PLANE + y_block)
     c_dev = dev(x, z * PLANE + c_block)
     offsets = [(dx, dz) for dz in range(planes) for dx in range(experts) if dx or dz]
+    step = 1 - 2 * (z // 2)
+    far = (planes - 1) * (1 - z // 2)
+    middle = ((z + 1) // 2) % 2
+    targets = [far, far - step, far - 2 * step - middle * step]
 
     def peer(dx, dz):
         return lax.rem(x + dx, experts), lax.rem(z + dz, planes)
@@ -95,6 +100,10 @@
         pl.semaphore_signal(barrier, inc=1, device_id=other,
                             device_id_type=pl.DeviceIdType.MESH)
 
+    small = [pltpu.make_async_copy(src, dst, tsem.at[n]) for n, (src, dst) in enumerate(
+        ((ids_hbm, ids_ref), (slot_hbm, slot_ref), (mix_hbm, mix_ref), (tok_hbm, tok_ref)))]
+    for load in small:
+        load.start()
     loads = []
     for h in range(HALVES):
         part = pl.ds(h * half, half)
@@ -104,9 +113,9 @@
     for g in range(groups):
         loads.append(pltpu.make_async_copy(
             wd_hbm.at[0, pl.ds(g * depth, depth)], wd.at[g], wsem.at[2 * HALVES + g]))
-    for load in loads:
-        load.start()
-
+
+    for load in small[:3]:
+        load.wait()
     lanes = experts * chunk_count * CAP
     ids = jnp.concatenate([ids_ref[...]] * (128 // tok_rows), axis=1)
     places = jnp.concatenate([slot_ref[...]] * (128 // tok_rows), axis=1)
@@ -123,6 +132,7 @@
         table += jnp.where((ids_k == wide_row // CAP) & (places_k == wide_row % CAP), mix_k, 0.0)
     pick = pick[:, :chunk_count * tok_rows].astype(BF)
     table = table.T
+    small[3].wait()
     for h in range(HALVES):
         stack = jnp.concatenate(
             [tok_ref[:, h * half + j * chunk: h * half + (j + 1) * chunk].astype(F32)
@@ -133,12 +143,16 @@
     weight_cols = {(e, r): table[:tok_rows, e * CAP + r:e * CAP + r + 1]
                    for e in range(experts) for r in range(CAP)}
 
+    for load in loads:
+        load.start()
     pl.semaphore_wait(barrier, len(offsets) + 2)
 
     waits = []
     for h in range(HALVES):
-        for n, (dx, dz) in reversed(list(enumerate(offsets))):
-            px, pz = peer(dx, dz)
+        stops = [(lax.rem(x + dx, experts), pz) for pz in targets
+                 for dx in range(experts - 1, -1, -1)]
+        stops += [peer(dx, 0) for dx in range(1, experts)]
+        for n, (px, pz) in enumerate(stops):
             copy = rdma(obuf.at[h, px], ubuf.at[h, unit], s1s.at[h, n], s1r.at[h, unit],
                         dev(px, pz * PLANE + b))
             copy.start()
@@ -189,61 +203,74 @@
         gate = g_part if gate is None else gate + g_part
         up = u_part if up is None else up + u_part
     hidden = (gate / (1.0 + jnp.exp(-gate)) * up).astype(BF)
-    hbuf[d] = hidden
+    piece = hbuf.shape[3]
+    for i in range(PARTS):
+        hbuf[d, i] = hidden[:, i * piece:(i + 1) * piece]
 
     def dp_of(zz, blk):
         return zz * PLANE + blk
 
-    shard = hbuf.at[d]
-    for dz in range(planes - 1, 0, -1):
-        pz = lax.rem(z + dz, planes)
-        copy = rdma(shard, shard, azs.at[dz], azr.at[z], dev(x, dp_of(pz, b)))
+    def send(g, i, ssem, rsem, device):
+        ref = hbuf.at[g, i]
+        copy = rdma(ref, ref, ssem, rsem, device)
         copy.start()
         waits.append(copy)
-    copy = rdma(shard, shard, ays.at[0], ayr.at[z], y_dev)
-    copy.start()
-    waits.append(copy)
-    copy = rdma(shard, shard, acs.at[0], acr.at[z, 0], c_dev)
-    copy.start()
-    waits.append(copy)
+
+    def receive(g, i, rsem):
+        ref = hbuf.at[g, i]
+        rdma(ref, ref, acs.at[0, 0], rsem, y_dev).wait_recv()
+
+    for i in range(PARTS):
+        send(d, i, ays.at[0, i], ayr.at[z, i], y_dev)
+        for n, pz in enumerate(targets):
+            send(d, i, azs.at[n, i], azr.at[z, i], dev(x, dp_of(pz, b)))
+        send(d, i, acs.at[0, i], acr.at[z, 0, i], c_dev)
     for load in loads[2 * HALVES:]:
         load.wait()
 
-    def product(g):
-        return jnp.dot(hbuf[g], wd[g], preferred_element_type=F32)
-
-    acc = product(d)
-    for dz in range(planes):
-        pz = lax.rem(z + dz, planes)
-        if dz:
+    def product(g, i):
+        return jnp.dot(hbuf[g, i], wd[g, i * piece:(i + 1) * piece],
+                       preferred_element_type=F32)
+
+    acc = None
+    for i in range(PARTS):
+        acc = product(d, i) if acc is None else acc + product(d, i)
+    near = [z] + targets[::-1]
+
+    def drain(i):
+        total = None
+        for n, pz in enumerate(near):
+            if n:
+                g = dp_of(pz, y_block)
+                receive(g, i, ayr.at[pz, i])
+                send(g, i, acs.at[planes + n, i], acr.at[pz, 1, i], c_dev)
+                term = product(g, i)
+                total = term if total is None else total + term
+        for n, pz in enumerate(near):
+            g = dp_of(pz, yc_block)
+            receive(g, i, acr.at[pz, 1, i])
+            total += product(g, i)
+        return total
+
+    for i in range(PARTS):
+        for n, pz in enumerate(near):
             g = dp_of(pz, b)
-            got = hbuf.at[g]
-            rdma(got, got, azs.at[dz], azr.at[pz], y_dev).wait_recv()
-            on_y = rdma(got, got, ays.at[dz], ayr.at[pz], y_dev)
-            on_y.start()
-            on_c = rdma(got, got, acs.at[dz], acr.at[pz, 0], c_dev)
-            on_c.start()
-            waits += [on_y, on_c]
-            acc += product(g)
-        g = dp_of(pz, c_block)
-        got = hbuf.at[g]
-        rdma(got, got, acs.at[0], acr.at[pz, 0], c_dev).wait_recv()
-        acc += product(g)
-    for dz in range(planes):
-        pz = lax.rem(z + dz, planes)
-        g = dp_of(pz, y_block)
-        got = hbuf.at[g]
-        rdma(got, got, ays.at[0], ayr.at[pz], y_dev).wait_recv()
-        on_c = rdma(got, got, acs.at[planes + dz], acr.at[pz, 1], c_dev)
-        on_c.start()
-        waits.append(on_c)
-        acc += product(g)
-    for dz in range(planes):
-        pz = lax.rem(z + dz, planes)
-        g = dp_of(pz, yc_block)
-        got = hbuf.at[g]
-        rdma(got, got, acs.at[0], acr.at[pz, 1], c_dev).wait_recv()
-        acc += product(g)
+            if n:
+                receive(g, i, azr.at[pz, i])
+                send(g, i, ays.at[n, i], ayr.at[pz, i], y_dev)
+                send(g, i, acs.at[n, i], acr.at[pz, 0, i], c_dev)
+                acc += product(g, i)
+            g = dp_of(pz, y_block)
+            if not n:
+                receive(g, i, ayr.at[pz, i])
+                send(g, i, acs.at[planes + n, i], acr.at[pz, 1, i], c_dev)
+                acc += product(g, i)
+            g = dp_of(pz, c_block)
+            receive(g, i, acr.at[pz, 0, i])
+            acc += product(g, i)
+        if i:
+            acc += drain(i - 1)
+    acc += drain(PARTS - 1)
 
     wide = cols // 128
     piece_rows = wide * CAP
@@ -298,26 +325,30 @@
     return pl.pallas_call(
         functools.partial(kernel, experts, groups),
         out_shape=jax.ShapeDtypeStruct((tok_rows, width), BF),
-        in_specs=[pl.BlockSpec(memory_space=pltpu.VMEM)] * 4
-        + [pl.BlockSpec(memory_space=pl.ANY)] * 3,
+        in_specs=[pl.BlockSpec(memory_space=pltpu.HBM)] * 7,
         out_specs=pl.BlockSpec(memory_space=pltpu.VMEM),
         scratch_shapes=[
+            pltpu.VMEM((tok_rows, width), BF),
+            pltpu.VMEM(expert_ids.shape[::-1], jnp.int32),
+            pltpu.VMEM(slots.shape[::-1], jnp.int32),
+            pltpu.VMEM(mix_weights.shape[::-1], F32),
+            dma((4,)),
             pltpu.VMEM((width, hid), BF),
             pltpu.VMEM((width, hid), BF),
             pltpu.VMEM((groups, hid, cols), BF),
             pltpu.VMEM((HALVES, experts, rows, chunk), BF),
             pltpu.VMEM((HALVES, units, rows, chunk), BF),
             pltpu.VMEM((HALVES, PLANE, rows, half), BF),
-            pltpu.VMEM((groups, PLANE * rows, hid), BF),
+            pltpu.VMEM((groups, PARTS, PLANE * rows, hid // PARTS), BF),
             pltpu.VMEM((everyone, cols // 128 * CAP, 128), BF),
             pltpu.VMEM((everyone, cols // 128 * CAP, 128), BF),
             dma((2 * HALVES + groups,)),
             dma((HALVES, units)), dma((HALVES, units)),
             dma((HALVES,)), dma((HALVES,)),
             dma((HALVES, 2)), dma((HALVES, 2)),
-            dma((planes,)), dma((planes,)),
-            dma((planes,)), dma((planes,)),
-            dma((2 * planes,)), dma((planes, 2)),
+            dma((planes, PARTS)), dma((planes, PARTS)),
+            dma((planes, PARTS)), dma((planes, PARTS)),
+            dma((2 * planes, PARTS)), dma((planes, 2, PARTS)),
             dma((everyone,)), dma((everyone,)),
         ],
         compiler_params=pltpu.CompilerParams(
@@ -334,10 +365,11 @@
         fits = (
             groups % PLANE == 0
             and rows == 16
+            and groups == 4 * PLANE
             and tokens.shape[0] == 8
             and experts * CAP <= 8
             and tokens.shape[1] % (HALVES * (rows // CAP) * 128) == 0
-            and w_gate.shape[2] % 128 == 0
+            and w_gate.shape[2] % (128 * PARTS) == 0
             and w_down.shape[2] % 128 == 0
         )
         form = kernel_form if fits else collective_form

time: 39.5 us -> 39 us (0.987)
  Pallas kernels: 37.8 us -> 37.3 us
    pallas_call x1, Pallas kernels: 37.8 us -> 37.3 us  [kernel_form(): pl.pallas_call(functools.partial(kernel, experts, groups), out_shape=jax....]
where the time goes in v3:
time: 39 us; the launch traced here: 38.8 us
  Pallas kernels  37.3 us (96%)
  local copies, waits for them, and re-layouts  1.47 us (4%)
    pallas_call x1, Pallas kernels, kernel_form(): pl.pallas_call(functools.partial(kernel, experts, groups), out_shape=jax....  37.3 us
    unnamed x1, local copies, waits for them, and re-layouts  1.47 us

profile of v3, /device:TPU:0, one launch (start us, length us, event | category | flops | bytes accessed | tf_op | source)
XLA Modules:
  0.0 38.8 jit_solution(17885238773837609467)
XLA Ops:
  0.0 37.3 %shard_map.73 = bf16[8,4096]{1,0:T(8,128)(2,1)} custom-call(bf16[8,4096]{1,0:T(8,128)(2,1)} %tok_hbm.1, s32[2,8]{1,0:T(2,128)} %bitcast.3, s32[2,8]{1,0:T(2,128)} %bitcast.4, f32[2,8]{1,0:T(2,128)} %bitcast.5, bf16[1,4096,512]{2,1,0:T(8,128)(2,1)} %wg_hbm.1, bf16[1,4096,512]{2,1,0:T(8,128)(2,1)} %wu_hbm.1, bf16[1,8192,256]{2,1,0:T(8,128)(2,1)} %wd_hbm.1), custom_call_target="tpu_custom_call" | custom-call | tf_op jit(solution)/shard_map/pallas_call | solution.py:325
  37.3 1.5 %copy.9 = bf16[8,4096]{1,0:T(8,128)(2,1)} copy(bf16[8,4096]{1,0:T(8,128)(2,1)} %shard_map.73) | data formatting | bytes 131072

commit v4 on v3

--- a/solution.py
+++ b/solution.py
@@ -10,7 +10,7 @@
 CAP = 2
 PLANE = 4
 PARTS = 1
-HALVES = 2
+HALVES = 1
 BF = jnp.bfloat16
 F32 = jnp.float32
 

time: 39 us -> 38.3 us (0.982)
  Pallas kernels: 37.3 us -> 36.6 us
    pallas_call x1, Pallas kernels: 37.3 us -> 36.6 us  [kernel_form(): pl.pallas_call(functools.partial(kernel, experts, groups), out_shape=jax....]
where the time goes in v4:
time: 38.3 us; the launch traced here: 38.1 us
  Pallas kernels  36.6 us (96%)
  local copies, waits for them, and re-layouts  1.47 us (4%)
    pallas_call x1, Pallas kernels, kernel_form(): pl.pallas_call(functools.partial(kernel, experts, groups), out_shape=jax....  36.6 us
    unnamed x1, local copies, waits for them, and re-layouts  1.47 us

profile of v4, /device:TPU:0, one launch (start us, length us, event | category | flops | bytes accessed | tf_op | source)
XLA Modules:
  0.0 38.1 jit_solution(11141886980626320994)
XLA Ops:
  0.0 36.6 %shard_map.73 = bf16[8,4096]{1,0:T(8,128)(2,1)} custom-call(bf16[8,4096]{1,0:T(8,128)(2,1)} %tok_hbm.1, s32[2,8]{1,0:T(2,128)} %bitcast.3, s32[2,8]{1,0:T(2,128)} %bitcast.4, f32[2,8]{1,0:T(2,128)} %bitcast.5, bf16[1,4096,512]{2,1,0:T(8,128)(2,1)} %wg_hbm.1, bf16[1,4096,512]{2,1,0:T(8,128)(2,1)} %wu_hbm.1, bf16[1,8192,256]{2,1,0:T(8,128)(2,1)} %wd_hbm.1), custom_call_target="tpu_custom_call" | custom-call | tf_op jit(solution)/shard_map/pallas_call | solution.py:325
  36.7 1.5 %copy.9 = bf16[8,4096]{1,0:T(8,128)(2,1)} copy(bf16[8,4096]{1,0:T(8,128)(2,1)} %shard_map.73) | data formatting | bytes 131072
